TPU v7x, 8 devices: a whole 2x2x1 slice. The times are simulated.
8 devices in a mesh: dp: 2 (over y, z), tp: 4 (over x, core).
Axes of the slice: x: 2, y: 2, z: 1, core: 2. Of those that a mesh axis runs over, the one named last changes fastest.
Arguments:
- x: bfloat16 [256, 5120], P('dp'), parts along dimension 0
- w_gate: bfloat16 [5120, 17920], P(None, 'tp')
- w_up: bfloat16 [5120, 17920], P(None, 'tp')
- w_down: bfloat16 [17920, 5120], P('tp')
Outputs:
- output: bfloat16 [256, 5120], P('dp'), parts along dimension 0
There are 2 independent parts. A program takes and returns all parts, laid end to end along the dimension named above; an argument that names none is the same for every part.
All inputs are finite; a program needn't handle non-finite values.
Results may differ from a plain program's by a relative error of at most 0.016.
Values are sent between devices in bfloat16 or wider.
A program may use at most 2 GiB of HBM per device.

v0:
```python
import jax
import jax.numpy as jnp
from jax import lax
from jax.sharding import PartitionSpec as P


def solution(mesh):
    def step(x, w_gate, w_up, w_down):
        gate = jnp.dot(x, w_gate, preferred_element_type=jnp.float32)
        up = jnp.dot(x, w_up, preferred_element_type=jnp.float32)
        hidden = (jax.nn.silu(gate) * up).astype(jnp.bfloat16)
        term = jnp.dot(hidden, w_down, preferred_element_type=jnp.float32).astype(jnp.bfloat16)
        return lax.psum(term, "tp")

    return jax.shard_map(
        step,
        mesh=mesh,
        in_specs=(P("dp", None), P(None, "tp"), P(None, "tp"), P("tp", None)),
        out_specs=P("dp", None),
        check_vma=False,
    )
```

profile of v0, /device:TPU:0, one launch (start us, length us, event | category | flops | bytes accessed | tf_op | source)
XLA Modules:
  0.0 105.6 jit_solution(10771316609319996545)
XLA Ops:
  6.5 0.0 copy-start
  6.5 0.0 all-reduce.2.cloned.1.call-start
  6.5 1.3 %copy-done = bf16[128,5120]{1,0:T(8,128)(2,1)S(1)} copy-done((bf16[128,5120]{1,0:T(8,128)(2,1)S(1)}, bf16[128,5120]{1,0:T(8,128)(2,1)}, u32[]{:S(2)}) %copy-start) | copy-done | bytes 1310744
  7.9 18.7 %fusion.8 = f32[128,4480]{1,0:T(8,128)} fusion(bf16[128,5120]{1,0:T(8,128)(2,1)S(1)} %copy-done, bf16[5120,4480]{1,0:T(8,128)(2,1)} %param.5), kind=kOutput, calls=%fused_computation.10 | convolution fusion | flops 5872025600 | bytes 49479680 | tf_op jit(solution)/shard_map/dot_general | solution.py:9
  26.6 32.9 %convolution_convert_fusion = bf16[128,5120]{1,0:T(8,128)(2,1)} fusion(bf16[4480,5120]{1,0:T(8,128)(2,1)} %param.7, bf16[128,5120]{1,0:T(8,128)(2,1)S(1)} %copy-done, bf16[5120,4480]{1,0:T(8,128)(2,1)} %param.6, f32[128,4480]{1,0:T(8,128)} %fusion.8), kind=kOutput, calls=%fused_computation.2 | convolution fusion | flops 11748147200 | bytes 96665600 | tf_op jit(solution)/shard_map/dot_general | solution.py:12
  59.5 0.0 all-reduce.2.cloned.1.call-update
  59.6 36.7 %all-reduce.2.cloned.1.call-done = bf16[128,5120]{1,0:T(8,128)(2,1)} async-done(((bf16[128,5120]{1,0:T(8,128)(2,1)}), bf16[128,5120]{1,0:T(8,128)(2,1)}) %all-reduce.2.cloned.1.call-update) | async-done | bytes 1310736 | tf_op jit(solution)/shard_map/psum | solution.py:13
  96.3 2.5 %copy.6 = bf16[128,5120]{1,0:T(8,128)(2,1)} copy(bf16[128,5120]{1,0:T(8,128)(2,1)} %all-reduce.2.cloned.1.call-done) | data formatting | bytes 2621440
Async XLA Ops:
  6.5 1.3 %copy-start = (bf16[128,5120]{1,0:T(8,128)(2,1)S(1)}, bf16[128,5120]{1,0:T(8,128)(2,1)}, u32[]{:S(2)}) copy-start(bf16[128,5120]{1,0:T(8,128)(2,1)} %param.4) | copy-start | bytes 3932164
  6.5 89.7 %all-reduce.2.cloned.1.call-start = ((), (), s32[]{:S(2)}) async-start(), calls=%async_computation | async-start | bytes 2621440 | tf_op jit(solution)/shard_map/psum | solution.py:13
Sparse Core Ops, SparseCore 0:
  59.7 36.5 all-reduce.1
where the time goes:
time: 106 us
  matrix products  51.7 us (49%)
  waiting for transfers between devices  36.7 us (35%)
  between operations  13.4 us (13%)
  local copies, waits for them, and re-layouts  3.77 us (4%)
    psum x1, waiting for transfers between devices, step(): return lax.psum(term, 'tp')  36.7 us
    dot_general x1, matrix products, step(): jnp.dot(hidden, w_down, preferred_element_type=jnp.float32)  32.9 us
    dot_general x1, matrix products, step(): gate = jnp.dot(x, w_gate, preferred_element_type=jnp.float32)  18.7 us
    unnamed x3, local copies, waits for them, and re-layouts  3.77 us
  transfers between devices with their start and end apart: 1, of which 1 were waited for; matrix products, arithmetic and copies ran while one was open for 0% of the time, Pallas kernels for 0%

commit v1 on v0

v1 whole, which is shorter than its diff:
```python
import jax
import jax.numpy as jnp
from jax import lax
from jax.experimental import pallas as pl
from jax.experimental.pallas import tpu as pltpu
from jax.sharding import PartitionSpec as P

MESH = pl.DeviceIdType.MESH
ROWS, D, FF = 128, 5120, 4480
U = 2304
SKIP = FF - U
KC = 512
NK = D // KC
NC = 512
NN = D // NC
HC = NC // 2
GS = 5
DS = 5
LAG_Y, LAG_X = 4, 6
F32, BF16 = jnp.float32, jnp.bfloat16


def kernel(x, wg, wu, wd, o, X, acc, h, gu, dn, mine, msend, mrecv, ysend, yrecv, xsend, xrecv,
           xsem, gsem, dsem, in_y, in_x, in_m, out_m, out_y, out_x, out_o):
    d, t = lax.axis_index("dp"), lax.axis_index("tp")
    xi, c = t // 2, t % 2
    mate, ypeer, xpeer = (d, t + 1 - 2 * c), (1 - d, t), (d, (t + 2) % 4)
    unit0 = pl.multiple_of(d * SKIP, 128)

    def remote(src, dst, sems, i, peer):
        return pltpu.make_async_remote_copy(
            src_ref=src, dst_ref=dst, send_sem=sems.at[0, i], recv_sem=sems.at[1, i], device_id=peer, device_id_type=MESH)

    def chunk(i):
        pair = (i - 2) // 2
        j = jnp.where(i < 2, i, jnp.where(i < 8, jnp.where(i % 2 == 0, pair + 2, pair), i - 5))
        relayed = jnp.where(i < 8, jnp.where(i < 2, 0, i % 2), 1)
        return 2 * j + jnp.where(relayed == 1, 1 - xi, xi)

    def x_own(k):
        return pltpu.make_async_copy(x.at[:, pl.ds(k * KC, KC)], X.at[k, pl.ds(0, ROWS)], xsem.at[k])

    def slab(i, which):
        w = (wg, wu)[which]
        rows = pl.ds(pl.multiple_of(chunk(i) * KC, KC), KC)
        s = i % GS
        return pltpu.make_async_copy(w.at[rows, pl.ds(unit0, U)], gu.at[s, which], gsem.at[s, which])

    def down(n, half):
        s = n % DS
        cols = pl.ds(pl.multiple_of(n * NC + jnp.where(half == 0, c, 1 - c) * HC, HC), HC)
        return pltpu.make_async_copy(
            wd.at[pl.ds(unit0, U), cols], dn.at[s, :, pl.ds(half * HC, HC)], dsem.at[s, half])

    def other(k, core):
        return X.at[k, pl.ds(ROWS, ROWS), pl.ds(pl.multiple_of(core * (KC // 2), KC // 2), KC // 2)]

    def mine_x(k):
        return X.at[k, pl.ds(0, ROWS), pl.ds(pl.multiple_of(c * (KC // 2), KC // 2), KC // 2)]

    def send_y(j):
        return remote(mine_x(2 * j + xi), other(2 * j + xi, c), in_y, j, ypeer)

    def relay_x(j):
        return remote(other(2 * j + xi, c), other(2 * j + xi, c), in_x, j, xpeer)

    def got_x(j):
        return remote(other(2 * j + 1 - xi, c), other(2 * j + 1 - xi, c), in_x, j, xpeer)

    def to_mate(j, relayed):
        k = 2 * j + (1 - xi if relayed else xi)
        return remote(other(k, c), other(k, c), in_m, j + 5 * relayed, mate)

    def from_mate(j, relayed):
        k = 2 * j + (1 - xi if relayed else xi)
        return remote(other(k, 1 - c), other(k, 1 - c), in_m, j + 5 * relayed, mate)

    for k in range(NK):
        x_own(k).start()
    for i in range(GS):
        slab(i, 0).start()
        slab(i, 1).start()
    barrier = pltpu.get_barrier_semaphore()
    for peer in (mate, ypeer, xpeer):
        pl.semaphore_signal(barrier, inc=1, device_id=peer, device_id_type=MESH)
    pl.semaphore_wait(barrier, 3)
    for k in range(NK):
        x_own(k).wait()
    for j in range(5):
        send_y(j).start()
    acc[...] = jnp.zeros_like(acc)
    for n in range(DS):
        down(n, 0).start()
        down(n, 1).start()

    def direct(j):
        send_y(j).wait_recv()
        relay_x(j).start()
        to_mate(j, 0).start()

    direct(0)

    @pl.loop(0, NK)
    def _(i):
        @pl.when(i < 4)
        def _():
            direct(i + 1)

        @pl.when(jnp.logical_and(i >= 2, i < 7))
        def _():
            got_x(i - 2).wait_recv()
            to_mate(i - 2, 1).start()

        @pl.when(i < 2)
        def _():
            from_mate(i, 0).wait_recv()

        @pl.when(jnp.logical_and(i >= 2, i < 8))
        def _():
            @pl.when(i % 2 == 0)
            def _():
                from_mate((i - 2) // 2 + 2, 0).wait_recv()

            @pl.when(i % 2 == 1)
            def _():
                from_mate((i - 2) // 2, 1).wait_recv()

        @pl.when(i >= 8)
        def _():
            from_mate(i - 5, 1).wait_recv()

        k = chunk(i)
        s = i % GS
        xk = X[k]
        for which in range(2):
            slab(i, which).wait()
            acc[:, which * U:(which + 1) * U] += jnp.dot(xk, gu[s, which], preferred_element_type=F32)

            @pl.when(i + GS < NK)
            def _():
                slab(i + GS, which).start()

    @pl.loop(0, U // 256)
    def _(b):
        g = acc[:, pl.ds(pl.multiple_of(b * 256, 256), 256)]
        u = acc[:, pl.ds(pl.multiple_of(U + b * 256, 256), 256)]
        h[:, pl.ds(pl.multiple_of(b * 256, 256), 256)] = (jax.nn.silu(g) * u).astype(BF16)

    @pl.when(d == 1)
    def _():
        h[:, 0:2 * U - FF] = jnp.zeros((2 * ROWS, 2 * U - FF), BF16)

    def swap(n):
        return remote(msend.at[n], mrecv.at[n], out_m, n, mate)

    def cross_y(n):
        return remote(ysend.at[n], yrecv.at[n], out_y, n, ypeer)

    def cross_x(n):
        return remote(xsend.at[n], xrecv.at[n], out_x, n, xpeer)

    def give(n, core):
        cols = pl.ds(pl.multiple_of(n * NC + core * HC, HC), HC)
        return remote(o.at[:, cols], o.at[:, cols], out_o, n, mate)

    @pl.loop(0, NN + LAG_X)
    def _(n):
        @pl.when(n < NN)
        def _():
            s = n % DS
            down(n, 0).wait()
            down(n, 1).wait()
            p = jnp.dot(h[...], dn[s], preferred_element_type=F32)
            mine[n] = p[:, :HC]
            msend[n] = p[:, HC:].astype(BF16)
            swap(n).start()

            @pl.when(n + DS < NN)
            def _():
                down(n + DS, 0).start()
                down(n + DS, 1).start()

        @pl.when(jnp.logical_and(n >= 1, n < NN + 1))
        def _():
            m = n - 1
            swap(m).wait_recv()
            both = mine[m] + mrecv[m].astype(F32)
            ysend[m] = both[ROWS:].astype(BF16)
            mine[m, pl.ds(0, ROWS)] = both[:ROWS]
            cross_y(m).start()

        @pl.when(jnp.logical_and(n >= LAG_Y, n < NN + LAG_Y))
        def _():
            m = n - LAG_Y
            cross_y(m).wait_recv()
            xsend[m] = (mine[m, pl.ds(0, ROWS)] + yrecv[m].astype(F32)).astype(BF16)
            cross_x(m).start()

        @pl.when(n >= LAG_X)
        def _():
            m = n - LAG_X
            cross_x(m).wait_recv()
            cols = pl.ds(pl.multiple_of(m * NC + c * HC, HC), HC)
            o[:, cols] = (xsend[m].astype(F32) + xrecv[m].astype(F32)).astype(BF16)
            give(m, c).start()

    for j in range(5):
        send_y(j).wait_send()
        relay_x(j).wait_send()
        to_mate(j, 0).wait_send()
        to_mate(j, 1).wait_send()

    @pl.loop(0, NN)
    def _(n):
        swap(n).wait_send()
        cross_y(n).wait_send()
        cross_x(n).wait_send()
        give(n, c).wait_send()
        give(n, 1 - c).wait_recv()


def solution(mesh):
    dma = pltpu.SemaphoreType.DMA
    vmem = pltpu.VMEM

    def step(x, w_gate, w_up, w_down):
        return pl.pallas_call(
            kernel,
            out_shape=jax.ShapeDtypeStruct((ROWS, D), BF16),
            in_specs=[pl.BlockSpec(memory_space=pl.ANY)] * 4,
            out_specs=pl.BlockSpec(memory_space=pltpu.VMEM),
            scratch_shapes=[
                vmem((NK, 2 * ROWS, KC), BF16),
                vmem((2 * ROWS, 2 * U), F32),
                vmem((2 * ROWS, U), BF16),
                vmem((GS, 2, KC, U), BF16),
                vmem((DS, U, NC), BF16),
                vmem((NN, 2 * ROWS, HC), F32),
                vmem((NN, 2 * ROWS, HC), BF16),
                vmem((NN, 2 * ROWS, HC), BF16),
                vmem((NN, ROWS, HC), BF16),
                vmem((NN, ROWS, HC), BF16),
                vmem((NN, ROWS, HC), BF16),
                vmem((NN, ROWS, HC), BF16),
                dma((NK,)),
                dma((GS, 2)),
                dma((DS, 2)),
                dma((2, 5)),
                dma((2, 5)),
                dma((2, 10)),
                dma((2, NN)),
                dma((2, NN)),
                dma((2, NN)),
                dma((2, NN)),
            ],
            compiler_params=pltpu.CompilerParams(
                collective_id=0, has_side_effects=True, vmem_limit_bytes=63 * 2**20),
        )(x, w_gate, w_up, w_down)

    return jax.shard_map(
        step,
        mesh=mesh,
        in_specs=(P("dp", None), P(None, "tp"), P(None, "tp"), P("tp", None)),
        out_specs=P("dp", None),
        check_vma=False,
    )
```

time: 106 us -> 60.5 us (0.57)
  Pallas kernels: 0 us -> 58 us
  matrix products: 51.7 us -> 0 us
  waiting for transfers between devices: 36.7 us -> 0 us
  between operations: 13.4 us -> 0.01 us
  local copies, waits for them, and re-layouts: 3.77 us -> 2.46 us
    pallas_call x0 -> x1, Pallas kernels: none -> 58 us  [step(): pl.pallas_call(kernel, out_shape=jax.ShapeDtypeStruct((ROWS, D), BF16), i...]
    dot_general x2 -> x0, matrix products: 51.7 us -> none  [the longest x1 32.9 us: step(): jnp.dot(hidden, w_down, preferred_element_type=jnp.float32)]
    psum x1 -> x0, waiting for transfers between devices: 36.7 us -> none  [step(): return lax.psum(term, 'tp')]
    unnamed x3 -> x1, local copies, waits for them, and re-layouts: 3.77 us -> 2.46 us
  transfers between devices with their start and end apart: 1 -> 0, of which waited for: 1 -> 0; matrix products, arithmetic and copies ran while one was open for 0% -> 0% of each run, Pallas kernels for 0% -> 0%
where the time goes in v1:
time: 60.5 us; the launch traced here: 60.4 us
  Pallas kernels  58 us (96%)
  local copies, waits for them, and re-layouts  2.46 us (4%)
    pallas_call x1, Pallas kernels, step(): pl.pallas_call(kernel, out_shape=jax.ShapeDtypeStruct((ROWS, D), BF16), i...  58 us
    unnamed x1, local copies, waits for them, and re-layouts  2.46 us

profile of v1, /device:TPU:0, one launch (start us, length us, event | category | flops | bytes accessed | tf_op | source)
XLA Modules:
  0.0 60.4 jit_solution(18067769079581591422)
XLA Ops:
  0.0 58.0 %shard_map.46 = bf16[128,5120]{1,0:T(8,128)(2,1)} custom-call(bf16[128,5120]{1,0:T(8,128)(2,1)} %x.1, bf16[5120,4480]{1,0:T(8,128)(2,1)} %wg.1, bf16[5120,4480]{1,0:T(8,128)(2,1)} %wu.1, bf16[4480,5120]{1,0:T(8,128)(2,1)} %wd.1), custom_call_target="tpu_custom_call" | custom-call | tf_op jit(solution)/shard_map/pallas_call | solution.py:227
  58.0 2.5 %copy.6 = bf16[128,5120]{1,0:T(8,128)(2,1)} copy(bf16[128,5120]{1,0:T(8,128)(2,1)} %shard_map.46) | data formatting | bytes 2621440

commit v2 on v1

--- a/solution.py
+++ b/solution.py
@@ -14,14 +14,14 @@
 NC = 512
 NN = D // NC
 HC = NC // 2
-GS = 5
-DS = 5
-LAG_Y, LAG_X = 4, 6
+GS = 6
+DS = 4
+LAG_Y, LAG_X = 5, 7
 F32, BF16 = jnp.float32, jnp.bfloat16
 
 
 def kernel(x, wg, wu, wd, o, X, acc, h, gu, dn, mine, msend, mrecv, ysend, yrecv, xsend, xrecv,
-           xsem, gsem, dsem, in_y, in_x, in_m, out_m, out_y, out_x, out_o):
+           fin, xsem, ksem, gsem, dsem, in_y, in_x, in_m, out_m, out_y, out_x, out_o):
     d, t = lax.axis_index("dp"), lax.axis_index("tp")
     xi, c = t // 2, t % 2
     mate, ypeer, xpeer = (d, t + 1 - 2 * c), (1 - d, t), (d, (t + 2) % 4)
@@ -78,67 +78,114 @@
     for k in range(NK):
         x_own(k).start()
     for i in range(GS):
-        slab(i, 0).start()
-        slab(i, 1).start()
+        slab(i, 0).start(priority=1)
+        slab(i, 1).start(priority=1)
     barrier = pltpu.get_barrier_semaphore()
     for peer in (mate, ypeer, xpeer):
         pl.semaphore_signal(barrier, inc=1, device_id=peer, device_id_type=MESH)
-    pl.semaphore_wait(barrier, 3)
-    for k in range(NK):
-        x_own(k).wait()
+    acc[...] = jnp.zeros_like(acc)
+    with jax.named_scope("bar"):
+        pl.semaphore_wait(barrier, 3)
+    with jax.named_scope("wxown"):
+        for k in range(NK):
+            x_own(k).wait()
     for j in range(5):
         send_y(j).start()
-    acc[...] = jnp.zeros_like(acc)
     for n in range(DS):
-        down(n, 0).start()
-        down(n, 1).start()
+        down(n, 0).start(priority=1)
+        down(n, 1).start(priority=1)
 
     def direct(j):
-        send_y(j).wait_recv()
+        with jax.named_scope("wdirect"):
+            send_y(j).wait_recv()
         relay_x(j).start()
         to_mate(j, 0).start()
 
-    direct(0)
-
-    @pl.loop(0, NK)
+    def relayed(j):
+        with jax.named_scope("wrelay"):
+            got_x(j).wait_recv()
+        to_mate(j, 1).start()
+
+    def whole(j, was_relayed):
+        with jax.named_scope("wmate"):
+            from_mate(j, was_relayed).wait_recv()
+
+    def arrived(i):
+        with jax.named_scope("wslab"):
+            slab(i, 0).wait()
+            slab(i, 1).wait()
+
+    def free(i):
+        @pl.when(i + GS < NK)
+        def _():
+            slab(i + GS, 0).start(priority=1)
+            slab(i + GS, 1).start(priority=1)
+
+    def multiply(i, rows):
+        xk = X[chunk(i), rows]
+        with jax.named_scope("dot1"):
+            for which in range(2):
+                acc[rows, which * U:(which + 1) * U] += jnp.dot(xk, gu[i % GS, which], preferred_element_type=F32)
+
+    own, others, both = slice(0, ROWS), slice(ROWS, 2 * ROWS), slice(0, 2 * ROWS)
+
+    @pl.loop(0, 3)
     def _(i):
-        @pl.when(i < 4)
+        arrived(i)
+        multiply(i, own)
+
+        @pl.when(i == 1)
+        def _():
+            direct(0)
+
+    @pl.loop(0, 3)
+    def _(i):
+        @pl.when(i < 2)
         def _():
             direct(i + 1)
 
-        @pl.when(jnp.logical_and(i >= 2, i < 7))
-        def _():
-            got_x(i - 2).wait_recv()
-            to_mate(i - 2, 1).start()
-
-        @pl.when(i < 2)
-        def _():
-            from_mate(i, 0).wait_recv()
-
-        @pl.when(jnp.logical_and(i >= 2, i < 8))
-        def _():
-            @pl.when(i % 2 == 0)
-            def _():
-                from_mate((i - 2) // 2 + 2, 0).wait_recv()
-
-            @pl.when(i % 2 == 1)
-            def _():
-                from_mate((i - 2) // 2, 1).wait_recv()
-
-        @pl.when(i >= 8)
-        def _():
-            from_mate(i - 5, 1).wait_recv()
-
-        k = chunk(i)
-        s = i % GS
-        xk = X[k]
-        for which in range(2):
-            slab(i, which).wait()
-            acc[:, which * U:(which + 1) * U] += jnp.dot(xk, gu[s, which], preferred_element_type=F32)
-
-            @pl.when(i + GS < NK)
-            def _():
-                slab(i + GS, which).start()
+        @pl.when(i == 2)
+        def _():
+            relayed(0)
+
+        whole(i, 0)
+        multiply(i, others)
+        free(i)
+
+    @pl.loop(3, NK)
+    def _(i):
+        @pl.when(i < 5)
+        def _():
+            direct(i)
+            relayed(i - 2)
+
+        @pl.when(jnp.logical_and(i >= 5, i < 7))
+        def _():
+            relayed(i - 2)
+
+        @pl.when(i % 2 == 1)
+        def _():
+            @pl.when(i < 9)
+            def _():
+                whole((i - 3) // 2, 1)
+
+            @pl.when(i == 9)
+            def _():
+                whole(4, 1)
+
+        @pl.when(i % 2 == 0)
+        def _():
+            @pl.when(i < 8)
+            def _():
+                whole(i // 2 + 1, 0)
+
+            @pl.when(i == 8)
+            def _():
+                whole(3, 1)
+
+        arrived(i)
+        multiply(i, both)
+        free(i)
 
     @pl.loop(0, U // 256)
     def _(b):
@@ -161,29 +208,35 @@
 
     def give(n, core):
         cols = pl.ds(pl.multiple_of(n * NC + core * HC, HC), HC)
-        return remote(o.at[:, cols], o.at[:, cols], out_o, n, mate)
+        return remote(fin.at[n], o.at[:, cols], out_o, n, mate)
+
+    def keep(n):
+        return pltpu.make_async_copy(fin.at[n], o.at[:, pl.ds(pl.multiple_of(n * NC + c * HC, HC), HC)], ksem.at[n])
 
     @pl.loop(0, NN + LAG_X)
     def _(n):
         @pl.when(n < NN)
         def _():
             s = n % DS
-            down(n, 0).wait()
-            down(n, 1).wait()
-            p = jnp.dot(h[...], dn[s], preferred_element_type=F32)
+            with jax.named_scope('wdown'):
+                down(n, 0).wait()
+                down(n, 1).wait()
+            with jax.named_scope('dot2'):
+                p = jnp.dot(h[...], dn[s], preferred_element_type=F32)
             mine[n] = p[:, :HC]
             msend[n] = p[:, HC:].astype(BF16)
             swap(n).start()
 
             @pl.when(n + DS < NN)
             def _():
-                down(n + DS, 0).start()
-                down(n + DS, 1).start()
+                down(n + DS, 0).start(priority=1)
+                down(n + DS, 1).start(priority=1)
 
         @pl.when(jnp.logical_and(n >= 1, n < NN + 1))
         def _():
             m = n - 1
-            swap(m).wait_recv()
+            with jax.named_scope('wswap'):
+                swap(m).wait_recv()
             both = mine[m] + mrecv[m].astype(F32)
             ysend[m] = both[ROWS:].astype(BF16)
             mine[m, pl.ds(0, ROWS)] = both[:ROWS]
@@ -192,17 +245,19 @@
         @pl.when(jnp.logical_and(n >= LAG_Y, n < NN + LAG_Y))
         def _():
             m = n - LAG_Y
-            cross_y(m).wait_recv()
+            with jax.named_scope('wy'):
+                cross_y(m).wait_recv()
             xsend[m] = (mine[m, pl.ds(0, ROWS)] + yrecv[m].astype(F32)).astype(BF16)
             cross_x(m).start()
 
         @pl.when(n >= LAG_X)
         def _():
             m = n - LAG_X
-            cross_x(m).wait_recv()
-            cols = pl.ds(pl.multiple_of(m * NC + c * HC, HC), HC)
-            o[:, cols] = (xsend[m].astype(F32) + xrecv[m].astype(F32)).astype(BF16)
+            with jax.named_scope('wx'):
+                cross_x(m).wait_recv()
+            fin[m] = (xsend[m].astype(F32) + xrecv[m].astype(F32)).astype(BF16)
             give(m, c).start()
+            keep(m).start()
 
     for j in range(5):
         send_y(j).wait_send()
@@ -215,6 +270,7 @@
         swap(n).wait_send()
         cross_y(n).wait_send()
         cross_x(n).wait_send()
+        keep(n).wait()
         give(n, c).wait_send()
         give(n, 1 - c).wait_recv()
 
@@ -228,7 +284,7 @@
             kernel,
             out_shape=jax.ShapeDtypeStruct((ROWS, D), BF16),
             in_specs=[pl.BlockSpec(memory_space=pl.ANY)] * 4,
-            out_specs=pl.BlockSpec(memory_space=pltpu.VMEM),
+            out_specs=pl.BlockSpec(memory_space=pl.ANY),
             scratch_shapes=[
                 vmem((NK, 2 * ROWS, KC), BF16),
                 vmem((2 * ROWS, 2 * U), F32),
@@ -242,7 +298,9 @@
                 vmem((NN, ROWS, HC), BF16),
                 vmem((NN, ROWS, HC), BF16),
                 vmem((NN, ROWS, HC), BF16),
+                vmem((NN, ROWS, HC), BF16),
                 dma((NK,)),
+                dma((NN,)),
                 dma((GS, 2)),
                 dma((DS, 2)),
                 dma((2, 5)),

time: 60.5 us -> 51.4 us (0.85)
  Pallas kernels: 58 us -> 48.8 us
    pallas_call x1, Pallas kernels: 58 us -> 48.8 us  [step(): pl.pallas_call(kernel, out_shape=jax.ShapeDtypeStruct((ROWS, D), BF16), i...]
where the time goes in v2:
time: 51.4 us; the launch traced here: 51.3 us
  Pallas kernels  48.8 us (95%)
  local copies, waits for them, and re-layouts  2.46 us (5%)
    pallas_call x1, Pallas kernels, step(): pl.pallas_call(kernel, out_shape=jax.ShapeDtypeStruct((ROWS, D), BF16), i...  48.8 us
    unnamed x1, local copies, waits for them, and re-layouts  2.46 us

profile of v2, /device:TPU:0, one launch (start us, length us, event | category | flops | bytes accessed | tf_op | source)
XLA Modules:
  0.0 51.3 jit_solution(8764473295324379514)
XLA Ops:
  0.0 48.8 %shard_map.46 = bf16[128,5120]{1,0:T(8,128)(2,1)} custom-call(bf16[128,5120]{1,0:T(8,128)(2,1)} %x.1, bf16[5120,4480]{1,0:T(8,128)(2,1)} %wg.1, bf16[5120,4480]{1,0:T(8,128)(2,1)} %wu.1, bf16[4480,5120]{1,0:T(8,128)(2,1)} %wd.1), custom_call_target="tpu_custom_call" | custom-call | tf_op jit(solution)/shard_map/pallas_call | solution.py:283
  48.8 2.5 %copy.6 = bf16[128,5120]{1,0:T(8,128)(2,1)} copy(bf16[128,5120]{1,0:T(8,128)(2,1)} %shard_map.46) | data formatting | bytes 2621440

commit v3 on v0

v3 whole, which is shorter than its diff:
```python
import jax
import jax.numpy as jnp
from jax import lax
from jax.experimental import pallas as pl
from jax.experimental.pallas import tpu as pltpu
from jax.sharding import PartitionSpec as P

MESH = pl.DeviceIdType.MESH
ROWS, D, FF = 128, 5120, 4480
U = 2304
SKIP = FF - U
KC = 512
NK = D // KC
NC = 512
NN = D // NC
HC = NC // 2
GS = 6
DS = 5
LAG_O, LAG_Y, LAG_X = 2, 3, 6
F32, BF16 = jnp.float32, jnp.bfloat16


def kernel(x, wg, wu, wd, o, xs, acc, h, gu, dn, xkeep, okeep, xpart, xgot, opart, ogot, ysend, yrecv, xsend, xrecv,
           xsem, gsem, dsem, in_y, in_x, in_m, sx, so, out_y, out_x, out_o):
    d, t = lax.axis_index("dp"), lax.axis_index("tp")
    xi, c = t // 2, t % 2
    mate, ypeer, xpeer = (d, t + 1 - 2 * c), (1 - d, t), (d, (t + 2) % 4)
    unit0 = pl.multiple_of(d * SKIP, 128)

    def remote(src, dst, sems, i, peer):
        return pltpu.make_async_remote_copy(
            src_ref=src, dst_ref=dst, send_sem=sems.at[sems.shape[0] - 1], recv_sem=sems.at[i],
            device_id=peer, device_id_type=MESH)

    def all_sent(sems):
        n = sems.shape[0] - 1
        pltpu.make_async_copy(xpart.at[pl.ds(0, n)], xpart.at[pl.ds(0, n)], sems.at[n]).wait()

    def chunk(i):
        pair = (i - 2) // 2
        j = jnp.where(i < 2, i, jnp.where(i < 8, jnp.where(i % 2 == 0, pair + 2, pair), i - 5))
        relayed = jnp.where(i < 8, jnp.where(i < 2, 0, i % 2), 1)
        return 2 * j + jnp.where(relayed == 1, 1 - xi, xi)

    def x_own(k):
        return pltpu.make_async_copy(x.at[:, pl.ds(k * KC, KC)], xs.at[k, pl.ds(0, ROWS)], xsem.at[0])

    def slab(i, which):
        w = (wg, wu)[which]
        rows = pl.ds(pl.multiple_of(chunk(i) * KC, KC), KC)
        s = i % GS
        return pltpu.make_async_copy(w.at[rows, pl.ds(unit0, U)], gu.at[s, which], gsem.at[s])

    def down(n, half):
        s = n % DS
        cols = pl.ds(pl.multiple_of(n * NC + jnp.where(half == 0, c, 1 - c) * HC, HC), HC)
        return pltpu.make_async_copy(
            wd.at[pl.ds(unit0, U), cols], dn.at[s, :, pl.ds(half * HC, HC)], dsem.at[s])

    def load(n):
        down(n, 0).start(priority=1)
        down(n, 1).start(priority=1)

    def other(k, core):
        return xs.at[k, pl.ds(ROWS, ROWS), pl.ds(pl.multiple_of(core * (KC // 2), KC // 2), KC // 2)]

    def mine_x(k):
        return xs.at[k, pl.ds(0, ROWS), pl.ds(pl.multiple_of(c * (KC // 2), KC // 2), KC // 2)]

    def send_y(j):
        return remote(mine_x(2 * j + xi), other(2 * j + xi, c), in_y, j, ypeer)

    def relay_x(j):
        return remote(other(2 * j + xi, c), other(2 * j + xi, c), in_x, j, xpeer)

    def got_x(j):
        return remote(other(2 * j + 1 - xi, c), other(2 * j + 1 - xi, c), in_x, j, xpeer)

    def to_mate(j, relayed):
        k = 2 * j + (1 - xi if relayed else xi)
        return remote(other(k, c), other(k, c), in_m, j + 5 * relayed, mate)

    def from_mate(j, relayed):
        k = 2 * j + (1 - xi if relayed else xi)
        return remote(other(k, 1 - c), other(k, 1 - c), in_m, j + 5 * relayed, mate)

    for k in range(NK):
        x_own(k).start()
    for i in range(GS):
        slab(i, 0).start(priority=1)
        slab(i, 1).start(priority=1)
    barrier = pltpu.get_barrier_semaphore()
    for peer in (mate, ypeer, xpeer):
        pl.semaphore_signal(barrier, inc=1, device_id=peer, device_id_type=MESH)
    acc[...] = jnp.zeros_like(acc)
    with jax.named_scope("bar"):
        pl.semaphore_wait(barrier, 3)
    with jax.named_scope("wxown"):
        pltpu.make_async_copy(x, o, xsem.at[0]).wait()
    for j in range(5):
        send_y(j).start()
    def direct(j):
        with jax.named_scope("wdirect"):
            send_y(j).wait_recv()
        relay_x(j).start()
        to_mate(j, 0).start()

    def relayed(j):
        with jax.named_scope("wrelay"):
            got_x(j).wait_recv()
        to_mate(j, 1).start()

    def whole(j, was_relayed):
        with jax.named_scope("wmate"):
            from_mate(j, was_relayed).wait_recv()

    here = set()

    def arrived(i):
        if i in here:
            return
        here.add(i)
        with jax.named_scope("wslab"):
            pltpu.make_async_copy(gu.at[i % GS], gu.at[i % GS], gsem.at[i % GS]).wait()

    def free(i):
        if i + GS < NK:
            slab(i + GS, 0).start(priority=1)
            slab(i + GS, 1).start(priority=1)

    def multiply(i, rows):
        xk = xs[chunk(i), rows]
        with jax.named_scope("dot1"):
            for which in range(2):
                acc[rows, which * U:(which + 1) * U] += jnp.dot(xk, gu[i % GS, which], preferred_element_type=F32)

    own, others, both = slice(0, ROWS), slice(ROWS, 2 * ROWS), slice(0, 2 * ROWS)
    relayed_ones = {3: 0, 5: 1, 7: 2, 8: 3, 9: 4}
    direct_ones = {0: 0, 1: 1, 2: 2, 4: 3, 6: 4}

    def complete(i):
        if i in relayed_ones:
            whole(relayed_ones[i], 1)
        else:
            whole(direct_ones[i], 0)

    def gate(rows):
        with jax.named_scope("silu"):
            @pl.loop(0, U // 256)
            def _(b):
                g = acc[rows, pl.ds(pl.multiple_of(b * 256, 256), 256)]
                u = acc[rows, pl.ds(pl.multiple_of(U + b * 256, 256), 256)]
                h[rows, pl.ds(pl.multiple_of(b * 256, 256), 256)] = (jax.nn.silu(g) * u).astype(BF16)

        @pl.when(d == 1)
        def _():
            h[rows, 0:2 * U - FF] = jnp.zeros((ROWS, 2 * U - FF), BF16)

    def O(*steps):
        for i in steps:
            arrived(i)
        for i in steps:
            multiply(i, own)

    def X(*steps):
        for i in steps:
            complete(i)
        for i in steps:
            arrived(i)
        for i in steps:
            multiply(i, others)

    def F(*steps):
        for i in steps:
            complete(i)
        for i in steps:
            arrived(i)
        for i in steps:
            multiply(i, both)

    def swap_x(n):
        return remote(xpart.at[n], xgot.at[n], sx, n, mate)

    def swap_o(n):
        return remote(opart.at[n], ogot.at[n], so, n, mate)

    def cross_y(n):
        return remote(ysend.at[n], yrecv.at[n], out_y, n, ypeer)

    def cross_x(n):
        return remote(xsend.at[n], xrecv.at[n], out_x, n, xpeer)

    def give(n, core):
        cols = pl.ds(pl.multiple_of(n * NC + core * HC, HC), HC)
        return remote(o.at[:, cols], o.at[:, cols], out_o, n, mate)

    def product(n, rows, keep, part, swap):
        with jax.named_scope("dot2"):
            p = jnp.dot(h[rows], dn[n % DS], preferred_element_type=F32)
            keep[n] = p[:, :HC]
            part[n] = p[:, HC:].astype(BF16)
        swap(n).start()

    def product_x(n):
        with jax.named_scope("wdown"):
            pltpu.make_async_copy(dn.at[n % DS], dn.at[n % DS], dsem.at[n % DS]).wait()
        product(n, others, xkeep, xpart, swap_x)

    def product_o(n):
        product(n, own, okeep, opart, swap_o)

        @pl.when(n + DS < NN)
        def _():
            load(n + DS)

    def pass_y(n):
        with jax.named_scope("wswap"):
            swap_x(n).wait_recv()
        ysend[n] = (xkeep[n] + xgot[n].astype(F32)).astype(BF16)
        cross_y(n).start()

    def pass_x(n):
        swap_o(n).wait_recv()
        with jax.named_scope("wy"):
            cross_y(n).wait_recv()
        xsend[n] = (okeep[n] + ogot[n].astype(F32) + yrecv[n].astype(F32)).astype(BF16)
        cross_x(n).start()

    def finish(n):
        with jax.named_scope("wx"):
            cross_x(n).wait_recv()
        cols = pl.ds(pl.multiple_of(n * NC + c * HC, HC), HC)
        o[:, cols] = (xsend[n].astype(F32) + xrecv[n].astype(F32)).astype(BF16)
        give(n, c).start()

    O(0)
    O(1)
    direct(0)
    O(2)
    direct(1)
    X(0)
    free(0)
    O(3)
    direct(2)
    X(1)
    free(1)
    relayed(0)
    X(2)
    free(2)
    direct(3)
    relayed(1)
    X(3)
    free(3)
    direct(4)
    F(4)
    relayed(2)
    F(5)
    relayed(3)
    F(6)
    load(0)
    relayed(4)
    X(7)
    load(1)
    X(8)
    load(2)
    X(9)
    load(3)
    load(4)
    gate(others)
    product_x(0)
    product_x(1)
    O(7)
    pass_y(0)
    pass_y(1)
    product_x(2)
    O(8)
    pass_y(2)
    O(9)
    gate(own)
    product_o(0)
    product_x(3)
    product_o(1)
    pass_x(0)

    @pl.loop(4, NN + LAG_X)
    def _(n):
        @pl.when(n < NN)
        def _():
            product_x(n)

        @pl.when(n < NN + 1)
        def _():
            pass_y(n - 1)

        @pl.when(n < NN + LAG_O)
        def _():
            product_o(n - LAG_O)

        @pl.when(n < NN + LAG_Y)
        def _():
            pass_x(n - LAG_Y)

        @pl.when(n >= LAG_X)
        def _():
            finish(n - LAG_X)

    with jax.named_scope("wgive"):
        @pl.loop(0, NN)
        def _(n):
            give(n, 1 - c).wait_recv()

    with jax.named_scope("wend"):
        for sems in (in_y, in_x, in_m, sx, so, out_y, out_x, out_o):
            all_sent(sems)


def solution(mesh):
    dma = pltpu.SemaphoreType.DMA
    vmem = pltpu.VMEM

    def step(x, w_gate, w_up, w_down):
        return pl.pallas_call(
            kernel,
            out_shape=pltpu.VMEM((ROWS, D), BF16),
            in_specs=[pl.BlockSpec(memory_space=pl.ANY)] * 4,
            out_specs=pl.BlockSpec(memory_space=pltpu.VMEM),
            scratch_shapes=[
                vmem((NK, 2 * ROWS, KC), BF16),
                vmem((2 * ROWS, 2 * U), F32),
                vmem((2 * ROWS, U), BF16),
                vmem((GS, 2, KC, U), BF16),
                vmem((DS, U, NC), BF16),
                vmem((NN, ROWS, HC), F32),
                vmem((NN, ROWS, HC), F32),
                *[vmem((NN, ROWS, HC), BF16)] * 8,
                dma((1,)),
                dma((GS,)),
                dma((DS,)),
                dma((6,)),
                dma((6,)),
                dma((11,)),
                *[dma((NN + 1,))] * 5,
            ],
            compiler_params=pltpu.CompilerParams(
                collective_id=0, has_side_effects=True, vmem_limit_bytes=60 * 2**20),
        )(x, w_gate, w_up, w_down)

    return jax.shard_map(
        step,
        mesh=mesh,
        in_specs=(P("dp", None), P(None, "tp"), P(None, "tp"), P("tp", None)),
        out_specs=P("dp", None),
        check_vma=False,
    )
```

time: 106 us -> 45.9 us (0.43)
  matrix products: 51.7 us -> 0 us
  Pallas kernels: 0 us -> 44.8 us
  waiting for transfers between devices: 36.7 us -> 0 us
  between operations: 13.4 us -> 0.01 us
  local copies, waits for them, and re-layouts: 3.77 us -> 1.06 us
    dot_general x2 -> x0, matrix products: 51.7 us -> none  [the longest x1 32.9 us: step(): jnp.dot(hidden, w_down, preferred_element_type=jnp.float32)]
    pallas_call x0 -> x1, Pallas kernels: none -> 44.8 us  [step(): pl.pallas_call(kernel, out_shape=pltpu.VMEM((ROWS, D), BF16), in_specs=[p...]
    psum x1 -> x0, waiting for transfers between devices: 36.7 us -> none  [step(): return lax.psum(term, 'tp')]
    unnamed x3 -> x1, local copies, waits for them, and re-layouts: 3.77 us -> 1.06 us
  transfers between devices with their start and end apart: 1 -> 0, of which waited for: 1 -> 0; matrix products, arithmetic and copies ran while one was open for 0% -> 0% of each run, Pallas kernels for 0% -> 0%
where the time goes in v3:
time: 45.9 us
  Pallas kernels  44.8 us (98%)
  local copies, waits for them, and re-layouts  1.06 us (2%)
    pallas_call x1, Pallas kernels, step(): pl.pallas_call(kernel, out_shape=pltpu.VMEM((ROWS, D), BF16), in_specs=[p...  44.8 us
    unnamed x1, local copies, waits for them, and re-layouts  1.06 us

profile of v3, /device:TPU:0, one launch (start us, length us, event | category | flops | bytes accessed | tf_op | source)
XLA Modules:
  0.0 45.9 jit_solution(1996909269288322342)
XLA Ops:
  0.0 44.8 %shard_map.46 = bf16[128,5120]{1,0:T(8,128)(2,1)S(1)} custom-call(bf16[128,5120]{1,0:T(8,128)(2,1)} %x.1, bf16[5120,4480]{1,0:T(8,128)(2,1)} %wg.1, bf16[5120,4480]{1,0:T(8,128)(2,1)} %wu.1, bf16[4480,5120]{1,0:T(8,128)(2,1)} %wd.1), custom_call_target="tpu_custom_call" | custom-call | tf_op jit(solution)/shard_map/pallas_call | solution.py:322
  44.8 1.1 %copy.6 = bf16[128,5120]{1,0:T(8,128)(2,1)} copy(bf16[128,5120]{1,0:T(8,128)(2,1)S(1)} %shard_map.46) | data formatting | bytes 2621440

commit v4 on v3

--- a/solution.py
+++ b/solution.py
@@ -15,8 +15,8 @@
 NN = D // NC
 HC = NC // 2
 GS = 6
-DS = 5
-LAG_O, LAG_Y, LAG_X = 2, 3, 6
+DS = 6
+LAG_Y, LAG_X = 3, 6
 F32, BF16 = jnp.float32, jnp.bfloat16
 
 
@@ -32,9 +32,9 @@
             src_ref=src, dst_ref=dst, send_sem=sems.at[sems.shape[0] - 1], recv_sem=sems.at[i],
             device_id=peer, device_id_type=MESH)
 
-    def all_sent(sems):
-        n = sems.shape[0] - 1
-        pltpu.make_async_copy(xpart.at[pl.ds(0, n)], xpart.at[pl.ds(0, n)], sems.at[n]).wait()
+    def all_sent(sems, blocks):
+        some = xpart.at[pl.ds(0, blocks)]
+        pltpu.make_async_copy(some, some, sems.at[sems.shape[0] - 1]).wait()
 
     def chunk(i):
         pair = (i - 2) // 2
@@ -49,7 +49,7 @@
         w = (wg, wu)[which]
         rows = pl.ds(pl.multiple_of(chunk(i) * KC, KC), KC)
         s = i % GS
-        return pltpu.make_async_copy(w.at[rows, pl.ds(unit0, U)], gu.at[s, which], gsem.at[s])
+        return pltpu.make_async_copy(w.at[rows, pl.ds(unit0, U)], gu.at[s, which], gsem.at[s, which])
 
     def down(n, half):
         s = n % DS
@@ -121,7 +121,8 @@
             return
         here.add(i)
         with jax.named_scope("wslab"):
-            pltpu.make_async_copy(gu.at[i % GS], gu.at[i % GS], gsem.at[i % GS]).wait()
+            slab(i, 0).wait()
+            slab(i, 1).wait()
 
     def free(i):
         if i + GS < NK:
@@ -144,13 +145,15 @@
         else:
             whole(direct_ones[i], 0)
 
-    def gate(rows):
-        with jax.named_scope("silu"):
-            @pl.loop(0, U // 256)
-            def _(b):
-                g = acc[rows, pl.ds(pl.multiple_of(b * 256, 256), 256)]
-                u = acc[rows, pl.ds(pl.multiple_of(U + b * 256, 256), 256)]
-                h[rows, pl.ds(pl.multiple_of(b * 256, 256), 256)] = (jax.nn.silu(g) * u).astype(BF16)
+    def last(i, rows):
+        xk = xs[chunk(i), rows]
+        with jax.named_scope("dot1last"):
+            for b in range(U // 256):
+                gate, up = (
+                    acc[rows, w * U + b * 256:w * U + (b + 1) * 256]
+                    + jnp.dot(xk, gu[i % GS, w, :, b * 256:(b + 1) * 256], preferred_element_type=F32)
+                    for w in range(2))
+                h[rows, b * 256:(b + 1) * 256] = (jax.nn.silu(gate) * up).astype(BF16)
 
         @pl.when(d == 1)
         def _():
@@ -161,6 +164,14 @@
             arrived(i)
         for i in steps:
             multiply(i, own)
+
+    def O_in_parts(i):
+        here.add(i)
+        xk = xs[chunk(i), own]
+        for which in range(2):
+            slab(i, which).wait()
+            with jax.named_scope("dot1h"):
+                acc[own, which * U:(which + 1) * U] += jnp.dot(xk, gu[i % GS, which], preferred_element_type=F32)
 
     def X(*steps):
         for i in steps:
@@ -184,51 +195,78 @@
     def swap_o(n):
         return remote(opart.at[n], ogot.at[n], so, n, mate)
 
-    def cross_y(n):
-        return remote(ysend.at[n], yrecv.at[n], out_y, n, ypeer)
-
-    def cross_x(n):
-        return remote(xsend.at[n], xrecv.at[n], out_x, n, xpeer)
+    def part(q):
+        return pl.ds(q * (ROWS // 2), ROWS // 2)
+
+    def cross_y(n, q):
+        return remote(ysend.at[n, part(q)], yrecv.at[n, part(q)], out_y, 2 * n + q, ypeer)
+
+    def cross_x(n, q):
+        return remote(xsend.at[n, part(q)], xrecv.at[n, part(q)], out_x, 2 * n + q, xpeer)
 
     def give(n, core):
         cols = pl.ds(pl.multiple_of(n * NC + core * HC, HC), HC)
         return remote(o.at[:, cols], o.at[:, cols], out_o, n, mate)
 
-    def product(n, rows, keep, part, swap):
-        with jax.named_scope("dot2"):
-            p = jnp.dot(h[rows], dn[n % DS], preferred_element_type=F32)
-            keep[n] = p[:, :HC]
-            part[n] = p[:, HC:].astype(BF16)
-        swap(n).start()
-
-    def product_x(n):
+    def loaded(n):
         with jax.named_scope("wdown"):
             pltpu.make_async_copy(dn.at[n % DS], dn.at[n % DS], dsem.at[n % DS]).wait()
-        product(n, others, xkeep, xpart, swap_x)
+
+    def more(n):
+        @pl.when(n + DS < NN)
+        def _():
+            load(n + DS)
+
+    def product_x(n):
+        loaded(n)
+        with jax.named_scope("dot2"):
+            p = jnp.dot(h[others], dn[n % DS], preferred_element_type=F32)
+            xkeep[n] = p[:, :HC]
+            xpart[n] = p[:, HC:].astype(BF16)
+        swap_x(n).start()
 
     def product_o(n):
-        product(n, own, okeep, opart, swap_o)
-
-        @pl.when(n + DS < NN)
-        def _():
-            load(n + DS)
+        with jax.named_scope("dot2"):
+            p = jnp.dot(h[own], dn[n % DS], preferred_element_type=F32)
+            okeep[n] = p[:, :HC]
+            opart[n] = p[:, HC:].astype(BF16)
+        swap_o(n).start()
+        more(n)
+
+    def products(n, m):
+        loaded(n)
+        with jax.named_scope("dot2b"):
+            p = jnp.dot(h[others], dn[n % DS], preferred_element_type=F32)
+            r = jnp.dot(h[own], dn[m % DS], preferred_element_type=F32)
+            xkeep[n] = p[:, :HC]
+            xpart[n] = p[:, HC:].astype(BF16)
+            okeep[m] = r[:, :HC]
+            opart[m] = r[:, HC:].astype(BF16)
+        swap_x(n).start()
+        swap_o(m).start()
+        more(m)
 
     def pass_y(n):
         with jax.named_scope("wswap"):
             swap_x(n).wait_recv()
         ysend[n] = (xkeep[n] + xgot[n].astype(F32)).astype(BF16)
-        cross_y(n).start()
-
-    def pass_x(n):
-        swap_o(n).wait_recv()
+        cross_y(n, 0).start()
+        cross_y(n, 1).start()
+
+    def pass_x(n, q):
+        if q == 0:
+            with jax.named_scope("wswapo"):
+                swap_o(n).wait_recv()
         with jax.named_scope("wy"):
-            cross_y(n).wait_recv()
-        xsend[n] = (okeep[n] + ogot[n].astype(F32) + yrecv[n].astype(F32)).astype(BF16)
-        cross_x(n).start()
+            cross_y(n, q).wait_recv()
+        r = part(q)
+        xsend[n, r] = (okeep[n, r] + ogot[n, r].astype(F32) + yrecv[n, r].astype(F32)).astype(BF16)
+        cross_x(n, q).start()
 
     def finish(n):
         with jax.named_scope("wx"):
-            cross_x(n).wait_recv()
+            cross_x(n, 0).wait_recv()
+            cross_x(n, 1).wait_recv()
         cols = pl.ds(pl.multiple_of(n * NC + c * HC, HC), HC)
         o[:, cols] = (xsend[n].astype(F32) + xrecv[n].astype(F32)).astype(BF16)
         give(n, c).start()
@@ -236,7 +274,7 @@
     O(0)
     O(1)
     direct(0)
-    O(2)
+    O_in_parts(2)
     direct(1)
     X(0)
     free(0)
@@ -248,11 +286,12 @@
     X(2)
     free(2)
     direct(3)
-    relayed(1)
     X(3)
     free(3)
+    relayed(1)
     direct(4)
-    F(4)
+    O(4)
+    X(4)
     relayed(2)
     F(5)
     relayed(3)
@@ -263,42 +302,44 @@
     load(1)
     X(8)
     load(2)
-    X(9)
-    load(3)
-    load(4)
-    gate(others)
+    complete(9)
+    arrived(9)
+    last(9, others)
+    for n in range(3, DS):
+        load(n)
     product_x(0)
+    O(7)
     product_x(1)
-    O(7)
     pass_y(0)
+    O(8)
+    product_x(2)
     pass_y(1)
-    product_x(2)
-    O(8)
+    last(9, own)
     pass_y(2)
-    O(9)
-    gate(own)
     product_o(0)
-    product_x(3)
-    product_o(1)
-    pass_x(0)
-
-    @pl.loop(4, NN + LAG_X)
+    products(3, 1)
+
+    @pl.loop(LAG_Y, NN + LAG_X)
     def _(n):
+        @pl.when(n < NN + LAG_Y)
+        def _():
+            pass_x(n - LAG_Y, 0)
+
+        @pl.when(n < NN - 1)
+        def _():
+            products(n + 1, n - 1)
+
+        @pl.when(jnp.logical_and(n >= NN - 1, n < NN + 1))
+        def _():
+            product_o(n - 1)
+
         @pl.when(n < NN)
         def _():
-            product_x(n)
-
-        @pl.when(n < NN + 1)
-        def _():
-            pass_y(n - 1)
-
-        @pl.when(n < NN + LAG_O)
-        def _():
-            product_o(n - LAG_O)
+            pass_y(n)
 
         @pl.when(n < NN + LAG_Y)
         def _():
-            pass_x(n - LAG_Y)
+            pass_x(n - LAG_Y, 1)
 
         @pl.when(n >= LAG_X)
         def _():
@@ -310,8 +351,10 @@
             give(n, 1 - c).wait_recv()
 
     with jax.named_scope("wend"):
-        for sems in (in_y, in_x, in_m, sx, so, out_y, out_x, out_o):
-            all_sent(sems)
+        for sems in (in_y, in_x):
+            all_sent(sems, 5)
+        for sems in (in_m, sx, so, out_y, out_x, out_o):
+            all_sent(sems, NN)
 
 
 def solution(mesh):
@@ -334,15 +377,17 @@
                 vmem((NN, ROWS, HC), F32),
                 *[vmem((NN, ROWS, HC), BF16)] * 8,
                 dma((1,)),
-                dma((GS,)),
+                dma((GS, 2)),
                 dma((DS,)),
                 dma((6,)),
                 dma((6,)),
                 dma((11,)),
-                *[dma((NN + 1,))] * 5,
+                *[dma((NN + 1,))] * 2,
+                *[dma((2 * NN + 1,))] * 2,
+                dma((NN + 1,)),
             ],
             compiler_params=pltpu.CompilerParams(
-                collective_id=0, has_side_effects=True, vmem_limit_bytes=60 * 2**20),
+                collective_id=0, has_side_effects=True, vmem_limit_bytes=61 * 2**20),
         )(x, w_gate, w_up, w_down)
 
     return jax.shard_map(

time: 45.9 us -> 45.5 us (level)
  no operation moved by 1% of the time
where the time goes in v4:
time: 45.5 us; the launch traced here: 45.4 us
  Pallas kernels  44.4 us (98%)
  local copies, waits for them, and re-layouts  1.06 us (2%)
    pallas_call x1, Pallas kernels, step(): pl.pallas_call(kernel, out_shape=pltpu.VMEM((ROWS, D), BF16), in_specs=[p...  44.4 us
    unnamed x1, local copies, waits for them, and re-layouts  1.06 us

profile of v4, /device:TPU:0, one launch (start us, length us, event | category | flops | bytes accessed | tf_op | source)
XLA Modules:
  0.0 45.4 jit_solution(15797934736138512690)
XLA Ops:
  0.0 44.4 %shard_map.46 = bf16[128,5120]{1,0:T(8,128)(2,1)S(1)} custom-call(bf16[128,5120]{1,0:T(8,128)(2,1)} %x.1, bf16[5120,4480]{1,0:T(8,128)(2,1)} %wg.1, bf16[5120,4480]{1,0:T(8,128)(2,1)} %wu.1, bf16[4480,5120]{1,0:T(8,128)(2,1)} %wd.1), custom_call_target="tpu_custom_call" | custom-call | tf_op jit(solution)/shard_map/pallas_call | solution.py:365
  44.4 1.1 %copy.6 = bf16[128,5120]{1,0:T(8,128)(2,1)} copy(bf16[128,5120]{1,0:T(8,128)(2,1)S(1)} %shard_map.46) | data formatting | bytes 2621440

commit v5 on v4

--- a/solution.py
+++ b/solution.py
@@ -17,6 +17,7 @@
 GS = 6
 DS = 6
 LAG_Y, LAG_X = 3, 6
+RING, RING_Y = 4, 7
 F32, BF16 = jnp.float32, jnp.bfloat16
 
 
@@ -49,7 +50,7 @@
         w = (wg, wu)[which]
         rows = pl.ds(pl.multiple_of(chunk(i) * KC, KC), KC)
         s = i % GS
-        return pltpu.make_async_copy(w.at[rows, pl.ds(unit0, U)], gu.at[s, which], gsem.at[s, which])
+        return pltpu.make_async_copy(w.at[rows, pl.ds(unit0, U)], gu.at[s, which], gsem.at[s])
 
     def down(n, half):
         s = n % DS
@@ -121,8 +122,7 @@
             return
         here.add(i)
         with jax.named_scope("wslab"):
-            slab(i, 0).wait()
-            slab(i, 1).wait()
+            pltpu.make_async_copy(gu.at[i % GS], gu.at[i % GS], gsem.at[i % GS]).wait()
 
     def free(i):
         if i + GS < NK:
@@ -165,14 +165,6 @@
         for i in steps:
             multiply(i, own)
 
-    def O_in_parts(i):
-        here.add(i)
-        xk = xs[chunk(i), own]
-        for which in range(2):
-            slab(i, which).wait()
-            with jax.named_scope("dot1h"):
-                acc[own, which * U:(which + 1) * U] += jnp.dot(xk, gu[i % GS, which], preferred_element_type=F32)
-
     def X(*steps):
         for i in steps:
             complete(i)
@@ -190,23 +182,23 @@
             multiply(i, both)
 
     def swap_x(n):
-        return remote(xpart.at[n], xgot.at[n], sx, n, mate)
+        return remote(xpart.at[n], xgot.at[n], sx, n % RING, mate)
 
     def swap_o(n):
-        return remote(opart.at[n], ogot.at[n], so, n, mate)
+        return remote(opart.at[n], ogot.at[n], so, n % RING, mate)
 
     def part(q):
         return pl.ds(q * (ROWS // 2), ROWS // 2)
 
     def cross_y(n, q):
-        return remote(ysend.at[n, part(q)], yrecv.at[n, part(q)], out_y, 2 * n + q, ypeer)
+        return remote(ysend.at[n, part(q)], yrecv.at[n, part(q)], out_y, 2 * (n % RING_Y) + q, ypeer)
 
     def cross_x(n, q):
         return remote(xsend.at[n, part(q)], xrecv.at[n, part(q)], out_x, 2 * n + q, xpeer)
 
-    def give(n, core):
-        cols = pl.ds(pl.multiple_of(n * NC + core * HC, HC), HC)
-        return remote(o.at[:, cols], o.at[:, cols], out_o, n, mate)
+    def give(n):
+        cols = pl.ds(pl.multiple_of(n * NC + c * HC, HC), HC)
+        return remote(o.at[:, cols], o.at[:, cols], out_o, 0, mate)
 
     def loaded(n):
         with jax.named_scope("wdown"):
@@ -269,12 +261,12 @@
             cross_x(n, 1).wait_recv()
         cols = pl.ds(pl.multiple_of(n * NC + c * HC, HC), HC)
         o[:, cols] = (xsend[n].astype(F32) + xrecv[n].astype(F32)).astype(BF16)
-        give(n, c).start()
+        give(n).start()
 
     O(0)
     O(1)
     direct(0)
-    O_in_parts(2)
+    O(2)
     direct(1)
     X(0)
     free(0)
@@ -308,12 +300,12 @@
     for n in range(3, DS):
         load(n)
     product_x(0)
+    product_x(1)
     O(7)
-    product_x(1)
     pass_y(0)
-    O(8)
     product_x(2)
     pass_y(1)
+    multiply(8, own)
     last(9, own)
     pass_y(2)
     product_o(0)
@@ -346,9 +338,7 @@
             finish(n - LAG_X)
 
     with jax.named_scope("wgive"):
-        @pl.loop(0, NN)
-        def _(n):
-            give(n, 1 - c).wait_recv()
+        pltpu.make_async_copy(xpart, xpart, out_o.at[0]).wait()
 
     with jax.named_scope("wend"):
         for sems in (in_y, in_x):
@@ -377,14 +367,15 @@
                 vmem((NN, ROWS, HC), F32),
                 *[vmem((NN, ROWS, HC), BF16)] * 8,
                 dma((1,)),
-                dma((GS, 2)),
+                dma((GS,)),
                 dma((DS,)),
                 dma((6,)),
                 dma((6,)),
                 dma((11,)),
-                *[dma((NN + 1,))] * 2,
-                *[dma((2 * NN + 1,))] * 2,
-                dma((NN + 1,)),
+                *[dma((RING + 1,))] * 2,
+                dma((2 * RING_Y + 1,)),
+                dma((2 * NN + 1,)),
+                dma((2,)),
             ],
             compiler_params=pltpu.CompilerParams(
                 collective_id=0, has_side_effects=True, vmem_limit_bytes=61 * 2**20),

time: 45.5 us -> 44.8 us (0.985)
  Pallas kernels: 44.4 us -> 43.7 us
    pallas_call x1, Pallas kernels: 44.4 us -> 43.7 us  [step(): pl.pallas_call(kernel, out_shape=pltpu.VMEM((ROWS, D), BF16), in_specs=[p...]
where the time goes in v5:
time: 44.8 us; the launch traced here: 44.7 us
  Pallas kernels  43.7 us (98%)
  local copies, waits for them, and re-layouts  1.06 us (2%)
    pallas_call x1, Pallas kernels, step(): pl.pallas_call(kernel, out_shape=pltpu.VMEM((ROWS, D), BF16), in_specs=[p...  43.7 us
    unnamed x1, local copies, waits for them, and re-layouts  1.06 us

profile of v5, /device:TPU:0, one launch (start us, length us, event | category | flops | bytes accessed | tf_op | source)
XLA Modules:
  0.0 44.7 jit_solution(12548937202103630825)
XLA Ops:
  0.0 43.7 %shard_map.46 = bf16[128,5120]{1,0:T(8,128)(2,1)S(1)} custom-call(bf16[128,5120]{1,0:T(8,128)(2,1)} %x.1, bf16[5120,4480]{1,0:T(8,128)(2,1)} %wg.1, bf16[5120,4480]{1,0:T(8,128)(2,1)} %wu.1, bf16[4480,5120]{1,0:T(8,128)(2,1)} %wd.1), custom_call_target="tpu_custom_call" | custom-call | tf_op jit(solution)/shard_map/pallas_call | solution.py:355
  43.7 1.1 %copy.6 = bf16[128,5120]{1,0:T(8,128)(2,1)} copy(bf16[128,5120]{1,0:T(8,128)(2,1)S(1)} %shard_map.46) | data formatting | bytes 2621440

commit v6 on v5

--- a/solution.py
+++ b/solution.py
@@ -14,10 +14,11 @@
 NC = 512
 NN = D // NC
 HC = NC // 2
+NB = NN + 1
 GS = 6
 DS = 6
 LAG_Y, LAG_X = 3, 6
-RING, RING_Y = 4, 7
+RING, RING_Y = 6, 8
 F32, BF16 = jnp.float32, jnp.bfloat16
 
 
@@ -54,7 +55,8 @@
 
     def down(n, half):
         s = n % DS
-        cols = pl.ds(pl.multiple_of(n * NC + jnp.where(half == 0, c, 1 - c) * HC, HC), HC)
+        first = jnp.where(n == NN - 1, half, jnp.where(half == 0, c, 1 - c))
+        cols = pl.ds(pl.multiple_of(n * NC + first * HC, HC), HC)
         return pltpu.make_async_copy(
             wd.at[pl.ds(unit0, U), cols], dn.at[s, :, pl.ds(half * HC, HC)], dsem.at[s])
 
@@ -145,6 +147,14 @@
         else:
             whole(direct_ones[i], 0)
 
+    def multiply_part(i, rows, core):
+        cut = pl.ds(pl.multiple_of(core * (KC // 2), KC // 2), KC // 2)
+        xk = xs[chunk(i), rows, cut]
+        with jax.named_scope("dot1p"):
+            for which in range(2):
+                acc[rows, which * U:(which + 1) * U] += jnp.dot(
+                    xk, gu[i % GS, which, cut], preferred_element_type=F32)
+
     def last(i, rows):
         xk = xs[chunk(i), rows]
         with jax.named_scope("dot1last"):
@@ -196,9 +206,12 @@
     def cross_x(n, q):
         return remote(xsend.at[n, part(q)], xrecv.at[n, part(q)], out_x, 2 * n + q, xpeer)
 
+    def columns(n):
+        start = jnp.where(n < NN - 1, n * NC + c * HC, (NN - 1) * NC + (n - NN + 1) * HC)
+        return pl.ds(pl.multiple_of(start, HC), HC)
+
     def give(n):
-        cols = pl.ds(pl.multiple_of(n * NC + c * HC, HC), HC)
-        return remote(o.at[:, cols], o.at[:, cols], out_o, 0, mate)
+        return remote(o.at[:, columns(n)], o.at[:, columns(n)], out_o, 0, mate)
 
     def loaded(n):
         with jax.named_scope("wdown"):
@@ -238,6 +251,37 @@
         swap_o(m).start()
         more(m)
 
+    def last_products(m):
+        loaded(NN - 1)
+        p = jnp.dot(h[others], dn[(NN - 1) % DS], preferred_element_type=F32)
+        r = jnp.dot(h[own], dn[m % DS], preferred_element_type=F32)
+        for i in range(2):
+            xkeep[NN - 1 + i] = p[:, i * HC:(i + 1) * HC]
+            xpart[NN - 1 + i] = p[:, i * HC:(i + 1) * HC].astype(BF16)
+        okeep[m] = r[:, :HC]
+        opart[m] = r[:, HC:].astype(BF16)
+        swap_o(m).start()
+
+        @pl.when(c == 0)
+        def _():
+            swap_x(NN - 1).start()
+            swap_x(NN).start()
+
+    def last_own_products(m):
+        r = jnp.dot(h[own], dn[m % DS], preferred_element_type=F32)
+        p = jnp.dot(h[own], dn[(NN - 1) % DS], preferred_element_type=F32)
+        okeep[m] = r[:, :HC]
+        opart[m] = r[:, HC:].astype(BF16)
+        for i in range(2):
+            okeep[NN - 1 + i] = p[:, i * HC:(i + 1) * HC]
+            opart[NN - 1 + i] = p[:, i * HC:(i + 1) * HC].astype(BF16)
+        swap_o(m).start()
+
+        @pl.when(c == 0)
+        def _():
+            swap_o(NN - 1).start()
+            swap_o(NN).start()
+
     def pass_y(n):
         with jax.named_scope("wswap"):
             swap_x(n).wait_recv()
@@ -259,16 +303,17 @@
         with jax.named_scope("wx"):
             cross_x(n, 0).wait_recv()
             cross_x(n, 1).wait_recv()
-        cols = pl.ds(pl.multiple_of(n * NC + c * HC, HC), HC)
-        o[:, cols] = (xsend[n].astype(F32) + xrecv[n].astype(F32)).astype(BF16)
+        o[:, columns(n)] = (xsend[n].astype(F32) + xrecv[n].astype(F32)).astype(BF16)
         give(n).start()
 
     O(0)
     O(1)
     direct(0)
+    multiply_part(0, others, c)
     O(2)
     direct(1)
-    X(0)
+    complete(0)
+    multiply_part(0, others, 1 - c)
     free(0)
     O(3)
     direct(2)
@@ -290,9 +335,13 @@
     F(6)
     load(0)
     relayed(4)
-    X(7)
     load(1)
-    X(8)
+    complete(7)
+    complete(8)
+    arrived(7)
+    arrived(8)
+    multiply(7, others)
+    multiply(8, others)
     load(2)
     complete(9)
     arrived(9)
@@ -307,44 +356,70 @@
     pass_y(1)
     multiply(8, own)
     last(9, own)
+    product_o(0)
     pass_y(2)
-    product_o(0)
     products(3, 1)
 
-    @pl.loop(LAG_Y, NN + LAG_X)
+    @pl.loop(LAG_Y, NN - 2)
     def _(n):
-        @pl.when(n < NN + LAG_Y)
-        def _():
-            pass_x(n - LAG_Y, 0)
-
-        @pl.when(n < NN - 1)
-        def _():
-            products(n + 1, n - 1)
-
-        @pl.when(jnp.logical_and(n >= NN - 1, n < NN + 1))
-        def _():
-            product_o(n - 1)
-
-        @pl.when(n < NN)
-        def _():
-            pass_y(n)
-
-        @pl.when(n < NN + LAG_Y)
-        def _():
-            pass_x(n - LAG_Y, 1)
+        pass_x(n - LAG_Y, 0)
+        products(n + 1, n - 1)
+        pass_y(n)
+        pass_x(n - LAG_Y, 1)
 
         @pl.when(n >= LAG_X)
         def _():
             finish(n - LAG_X)
 
-    with jax.named_scope("wgive"):
-        pltpu.make_async_copy(xpart, xpart, out_o.at[0]).wait()
-
-    with jax.named_scope("wend"):
-        for sems in (in_y, in_x):
-            all_sent(sems, 5)
-        for sems in (in_m, sx, so, out_y, out_x, out_o):
-            all_sent(sems, NN)
+    pass_x(NN - 5, 0)
+    last_products(NN - 3)
+    pass_y(NN - 2)
+    pass_x(NN - 5, 1)
+    finish(NN - 8)
+    pass_x(NN - 4, 0)
+    last_own_products(NN - 2)
+    pass_x(NN - 4, 1)
+
+    @pl.when(c == 1)
+    def _():
+        pass_y(NN - 1)
+        pass_y(NN)
+
+    finish(NN - 7)
+    for n in (NN - 3, NN - 2):
+        pass_x(n, 0)
+        pass_x(n, 1)
+        finish(n - 3)
+
+    @pl.when(c == 1)
+    def _():
+        for n in (NN - 1, NN):
+            pass_x(n, 0)
+            pass_x(n, 1)
+
+    for n in (NN - 4, NN - 3, NN - 2):
+        finish(n)
+
+    @pl.when(c == 1)
+    def _():
+        finish(NN - 1)
+        finish(NN)
+
+    for sems in (in_y, in_x):
+        all_sent(sems, 5)
+    all_sent(in_m, 10)
+    for core in range(2):
+        mine, gone = (NN - 1, NB) if core == 0 else (NB, NN - 1)
+
+        @pl.when(c == core)
+        def _():
+            with jax.named_scope("wgive"):
+                theirs = xpart.at[pl.ds(0, gone)]
+                pltpu.make_async_copy(theirs, theirs, out_o.at[0]).wait()
+            for sems in (sx, so):
+                all_sent(sems, gone)
+            for sems in (out_y, out_x, out_o):
+                all_sent(sems, mine)
 
 
 def solution(mesh):
@@ -363,9 +438,8 @@
                 vmem((2 * ROWS, U), BF16),
                 vmem((GS, 2, KC, U), BF16),
                 vmem((DS, U, NC), BF16),
-                vmem((NN, ROWS, HC), F32),
-                vmem((NN, ROWS, HC), F32),
-                *[vmem((NN, ROWS, HC), BF16)] * 8,
+                *[vmem((NB, ROWS, HC), F32)] * 2,
+                *[vmem((NB, ROWS, HC), BF16)] * 8,
                 dma((1,)),
                 dma((GS,)),
                 dma((DS,)),
@@ -374,7 +448,7 @@
                 dma((11,)),
                 *[dma((RING + 1,))] * 2,
                 dma((2 * RING_Y + 1,)),
-                dma((2 * NN + 1,)),
+                dma((2 * NB + 1,)),
                 dma((2,)),
             ],
             compiler_params=pltpu.CompilerParams(

time: 44.8 us -> 44.2 us (0.987)
  Pallas kernels: 43.7 us -> 43.1 us
    pallas_call x1, Pallas kernels: 43.7 us -> 43.1 us  [step(): pl.pallas_call(kernel, out_shape=pltpu.VMEM((ROWS, D), BF16), in_specs=[p...]
where the time goes in v6:
time: 44.2 us; the launch traced here: 44.1 us
  Pallas kernels  43.1 us (98%)
  local copies, waits for them, and re-layouts  1.06 us (2%)
    pallas_call x1, Pallas kernels, step(): pl.pallas_call(kernel, out_shape=pltpu.VMEM((ROWS, D), BF16), in_specs=[p...  43.1 us
    unnamed x1, local copies, waits for them, and re-layouts  1.06 us

profile of v6, /device:TPU:0, one launch (start us, length us, event | category | flops | bytes accessed | tf_op | source)
XLA Modules:
  0.0 44.1 jit_solution(7998064318735415232)
XLA Ops:
  0.0 43.1 %shard_map.46 = bf16[128,5120]{1,0:T(8,128)(2,1)S(1)} custom-call(bf16[128,5120]{1,0:T(8,128)(2,1)} %x.1, bf16[5120,4480]{1,0:T(8,128)(2,1)} %wg.1, bf16[5120,4480]{1,0:T(8,128)(2,1)} %wu.1, bf16[4480,5120]{1,0:T(8,128)(2,1)} %wd.1), custom_call_target="tpu_custom_call" | custom-call | tf_op jit(solution)/shard_map/pallas_call | solution.py:430
  43.1 1.1 %copy.6 = bf16[128,5120]{1,0:T(8,128)(2,1)} copy(bf16[128,5120]{1,0:T(8,128)(2,1)S(1)} %shard_map.46) | data formatting | bytes 2621440

commit v7 on v6

--- a/solution.py
+++ b/solution.py
@@ -222,8 +222,9 @@
         def _():
             load(n + DS)
 
-    def product_x(n):
-        loaded(n)
+    def product_x(n, here=False):
+        if not here:
+            loaded(n)
         with jax.named_scope("dot2"):
             p = jnp.dot(h[others], dn[n % DS], preferred_element_type=F32)
             xkeep[n] = p[:, :HC]
@@ -350,9 +351,10 @@
         load(n)
     product_x(0)
     product_x(1)
-    O(7)
+    loaded(2)
+    multiply(7, own)
+    product_x(2, True)
     pass_y(0)
-    product_x(2)
     pass_y(1)
     multiply(8, own)
     last(9, own)

time: 44.2 us -> 44.1 us (level)
  no operation moved by 1% of the time
where the time goes in v7:
time: 44.1 us; the launch traced here: 44 us
  Pallas kernels  43 us (98%)
  local copies, waits for them, and re-layouts  1.06 us (2%)
    pallas_call x1, Pallas kernels, step(): pl.pallas_call(kernel, out_shape=pltpu.VMEM((ROWS, D), BF16), in_specs=[p...  43 us
    unnamed x1, local copies, waits for them, and re-layouts  1.06 us

profile of v7, /device:TPU:0, one launch (start us, length us, event | category | flops | bytes accessed | tf_op | source)
XLA Modules:
  0.0 44.0 jit_solution(2650003366123168826)
XLA Ops:
  0.0 43.0 %shard_map.46 = bf16[128,5120]{1,0:T(8,128)(2,1)S(1)} custom-call(bf16[128,5120]{1,0:T(8,128)(2,1)} %x.1, bf16[5120,4480]{1,0:T(8,128)(2,1)} %wg.1, bf16[5120,4480]{1,0:T(8,128)(2,1)} %wu.1, bf16[4480,5120]{1,0:T(8,128)(2,1)} %wd.1), custom_call_target="tpu_custom_call" | custom-call | tf_op jit(solution)/shard_map/pallas_call | solution.py:432
  43.0 1.1 %copy.6 = bf16[128,5120]{1,0:T(8,128)(2,1)} copy(bf16[128,5120]{1,0:T(8,128)(2,1)S(1)} %shard_map.46) | data formatting | bytes 2621440

commit v8 on v7

--- a/solution.py
+++ b/solution.py
@@ -18,12 +18,12 @@
 GS = 6
 DS = 6
 LAG_Y, LAG_X = 3, 6
-RING, RING_Y = 6, 8
+RING, RING_Y, RING_X = 6, 8, 9
 F32, BF16 = jnp.float32, jnp.bfloat16
 
 
 def kernel(x, wg, wu, wd, o, xs, acc, h, gu, dn, xkeep, okeep, xpart, xgot, opart, ogot, ysend, yrecv, xsend, xrecv,
-           xsem, gsem, dsem, in_y, in_x, in_m, sx, so, out_y, out_x, out_o):
+           xsem, gsem, dsem, in_y, in_x, in_m, sx, so, out_y, out_x, out_o, sent):
     d, t = lax.axis_index("dp"), lax.axis_index("tp")
     xi, c = t // 2, t % 2
     mate, ypeer, xpeer = (d, t + 1 - 2 * c), (1 - d, t), (d, (t + 2) % 4)
@@ -31,12 +31,12 @@
 
     def remote(src, dst, sems, i, peer):
         return pltpu.make_async_remote_copy(
-            src_ref=src, dst_ref=dst, send_sem=sems.at[sems.shape[0] - 1], recv_sem=sems.at[i],
+            src_ref=src, dst_ref=dst, send_sem=sent.at[0], recv_sem=sems.at[i],
             device_id=peer, device_id_type=MESH)
 
-    def all_sent(sems, blocks):
-        some = xpart.at[pl.ds(0, blocks)]
-        pltpu.make_async_copy(some, some, sems.at[sems.shape[0] - 1]).wait()
+    def all_sent(blocks):
+        some = dn.at[pl.ds(0, 2), pl.ds(0, blocks * ROWS * HC // (2 * NC))]
+        pltpu.make_async_copy(some, some, sent.at[0]).wait()
 
     def chunk(i):
         pair = (i - 2) // 2
@@ -204,7 +204,7 @@
         return remote(ysend.at[n, part(q)], yrecv.at[n, part(q)], out_y, 2 * (n % RING_Y) + q, ypeer)
 
     def cross_x(n, q):
-        return remote(xsend.at[n, part(q)], xrecv.at[n, part(q)], out_x, 2 * n + q, xpeer)
+        return remote(xsend.at[n, part(q)], xrecv.at[n, part(q)], out_x, 2 * (n % RING_X) + q, xpeer)
 
     def columns(n):
         start = jnp.where(n < NN - 1, n * NC + c * HC, (NN - 1) * NC + (n - NN + 1) * HC)
@@ -335,19 +335,20 @@
     relayed(3)
     F(6)
     load(0)
+    load(1)
     relayed(4)
-    load(1)
+    load(2)
     complete(7)
     complete(8)
     arrived(7)
     arrived(8)
     multiply(7, others)
     multiply(8, others)
-    load(2)
+    load(3)
     complete(9)
     arrived(9)
     last(9, others)
-    for n in range(3, DS):
+    for n in range(4, DS):
         load(n)
     product_x(0)
     product_x(1)
@@ -407,9 +408,6 @@
         finish(NN - 1)
         finish(NN)
 
-    for sems in (in_y, in_x):
-        all_sent(sems, 5)
-    all_sent(in_m, 10)
     for core in range(2):
         mine, gone = (NN - 1, NB) if core == 0 else (NB, NN - 1)
 
@@ -418,10 +416,7 @@
             with jax.named_scope("wgive"):
                 theirs = xpart.at[pl.ds(0, gone)]
                 pltpu.make_async_copy(theirs, theirs, out_o.at[0]).wait()
-            for sems in (sx, so):
-                all_sent(sems, gone)
-            for sems in (out_y, out_x, out_o):
-                all_sent(sems, mine)
+            all_sent(20 + 2 * gone + 3 * mine)
 
 
 def solution(mesh):
@@ -445,13 +440,14 @@
                 dma((1,)),
                 dma((GS,)),
                 dma((DS,)),
-                dma((6,)),
-                dma((6,)),
-                dma((11,)),
-                *[dma((RING + 1,))] * 2,
-                dma((2 * RING_Y + 1,)),
-                dma((2 * NB + 1,)),
-                dma((2,)),
+                dma((5,)),
+                dma((5,)),
+                dma((10,)),
+                *[dma((RING,))] * 2,
+                dma((2 * RING_Y,)),
+                dma((2 * RING_X,)),
+                dma((1,)),
+                dma((1,)),
             ],
             compiler_params=pltpu.CompilerParams(
                 collective_id=0, has_side_effects=True, vmem_limit_bytes=61 * 2**20),

time: 44.1 us -> 44 us (level)
  no operation moved by 1% of the time
where the time goes in v8:
time: 44 us; the launch traced here: 43.9 us
  Pallas kernels  42.9 us (98%)
  local copies, waits for them, and re-layouts  1.06 us (2%)
    pallas_call x1, Pallas kernels, step(): pl.pallas_call(kernel, out_shape=pltpu.VMEM((ROWS, D), BF16), in_specs=[p...  42.9 us
    unnamed x1, local copies, waits for them, and re-layouts  1.06 us

profile of v8, /device:TPU:0, one launch (start us, length us, event | category | flops | bytes accessed | tf_op | source)
XLA Modules:
  0.0 43.9 jit_solution(8868387635445074489)
XLA Ops:
  0.0 42.9 %shard_map.46 = bf16[128,5120]{1,0:T(8,128)(2,1)S(1)} custom-call(bf16[128,5120]{1,0:T(8,128)(2,1)} %x.1, bf16[5120,4480]{1,0:T(8,128)(2,1)} %wg.1, bf16[5120,4480]{1,0:T(8,128)(2,1)} %wu.1, bf16[4480,5120]{1,0:T(8,128)(2,1)} %wd.1), custom_call_target="tpu_custom_call" | custom-call | tf_op jit(solution)/shard_map/pallas_call | solution.py:427
  42.9 1.1 %copy.6 = bf16[128,5120]{1,0:T(8,128)(2,1)} copy(bf16[128,5120]{1,0:T(8,128)(2,1)S(1)} %shard_map.46) | data formatting | bytes 2621440

commit v9 on v8

--- a/solution.py
+++ b/solution.py
@@ -16,7 +16,7 @@
 HC = NC // 2
 NB = NN + 1
 GS = 6
-DS = 6
+DS = 5
 LAG_Y, LAG_X = 3, 6
 RING, RING_Y, RING_X = 6, 8, 9
 F32, BF16 = jnp.float32, jnp.bfloat16
@@ -87,14 +87,14 @@
         k = 2 * j + (1 - xi if relayed else xi)
         return remote(other(k, 1 - c), other(k, 1 - c), in_m, j + 5 * relayed, mate)
 
+    barrier = pltpu.get_barrier_semaphore()
+    for peer in (mate, ypeer, xpeer):
+        pl.semaphore_signal(barrier, inc=1, device_id=peer, device_id_type=MESH)
     for k in range(NK):
         x_own(k).start()
     for i in range(GS):
         slab(i, 0).start(priority=1)
         slab(i, 1).start(priority=1)
-    barrier = pltpu.get_barrier_semaphore()
-    for peer in (mate, ypeer, xpeer):
-        pl.semaphore_signal(barrier, inc=1, device_id=peer, device_id_type=MESH)
     acc[...] = jnp.zeros_like(acc)
     with jax.named_scope("bar"):
         pl.semaphore_wait(barrier, 3)
@@ -261,12 +261,13 @@
             xpart[NN - 1 + i] = p[:, i * HC:(i + 1) * HC].astype(BF16)
         okeep[m] = r[:, :HC]
         opart[m] = r[:, HC:].astype(BF16)
-        swap_o(m).start()
 
         @pl.when(c == 0)
         def _():
             swap_x(NN - 1).start()
             swap_x(NN).start()
+
+        swap_o(m).start()
 
     def last_own_products(m):
         r = jnp.dot(h[own], dn[m % DS], preferred_element_type=F32)

time: 44 us -> 44 us (level)
  no operation moved by 1% of the time
where the time goes in v9:
time: 44 us; the launch traced here: 43.9 us
  Pallas kernels  42.8 us (97%)
  local copies, waits for them, and re-layouts  1.06 us (2%)
    pallas_call x1, Pallas kernels, step(): pl.pallas_call(kernel, out_shape=pltpu.VMEM((ROWS, D), BF16), in_specs=[p...  42.8 us
    unnamed x1, local copies, waits for them, and re-layouts  1.06 us

profile of v9, /device:TPU:0, one launch (start us, length us, event | category | flops | bytes accessed | tf_op | source)
XLA Modules:
  0.0 43.9 jit_solution(15619247353290500306)
XLA Ops:
  0.0 42.8 %shard_map.46 = bf16[128,5120]{1,0:T(8,128)(2,1)S(1)} custom-call(bf16[128,5120]{1,0:T(8,128)(2,1)} %x.1, bf16[5120,4480]{1,0:T(8,128)(2,1)} %wg.1, bf16[5120,4480]{1,0:T(8,128)(2,1)} %wu.1, bf16[4480,5120]{1,0:T(8,128)(2,1)} %wd.1), custom_call_target="tpu_custom_call" | custom-call | tf_op jit(solution)/shard_map/pallas_call | solution.py:428
  42.8 1.1 %copy.6 = bf16[128,5120]{1,0:T(8,128)(2,1)} copy(bf16[128,5120]{1,0:T(8,128)(2,1)S(1)} %shard_map.46) | data formatting | bytes 2621440
